TPU v7x, 32 devices: a whole 2x2x4 slice. The times are simulated.
32 devices in a mesh: section: 4 (over y, x), dp: 8 (over z, core).
Axes of the slice: x: 2, y: 2, z: 4, core: 2. Of those that a mesh axis runs over, the one named last changes fastest.
Arguments:
- token_ids: int32 [4, 512], P(None, 'dp'), may hold values from 0 to 127
- embed: bfloat16 [128, 512], replicated, may hold values from -6 to 6
- weights: bfloat16 [4, 2, 512, 2048], P('section'), may hold values from -0.25 to 0.25
- variance: bfloat16 [4, 1024, 2048], P('section', 'dp'), may hold values from 9.9658966e-05 to 0.0099487305
- momentum: bfloat16 [4, 1024, 2048], P('section', 'dp'), may hold values from -4 to 4
- worker_error: bfloat16 [4, 8, 2, 512, 2048], P('section', 'dp'), may hold values from -6 to 6
- server_error: float32 [4, 1024, 2048], P('section', 'dp'), may hold values from -0.75 to 0.75
- cotangent: bfloat16 [4, 512, 512], P(None, 'dp'), may hold values from -0.75 to 0.75
Outputs:
- new_weights: bfloat16 [4, 1024, 2048], P('section', 'dp')
- new_momentum: bfloat16 [4, 1024, 2048], P('section', 'dp')
- new_worker_error: bfloat16 [4, 8, 2, 512, 2048], P('section', 'dp')
- new_server_error: float32 [4, 1024, 2048], P('section', 'dp')
All inputs are finite; a program needn't handle non-finite values.
Results may differ from a plain program's by a relative error of at most 0.012.
Values may be sent and summed in bfloat16 or wider, within the bound.
A program may use at most 128 MiB of HBM per device.

v0:
```python
import math

import jax
import jax.numpy as jnp
from jax import lax
from jax.sharding import PartitionSpec as P

gelu_coef = math.sqrt(2.0 / math.pi)


def passed_along(array, axis, by):
    count = lax.axis_size(axis)
    pairs = [(i, i + by) for i in range(count) if 0 <= i + by < count]
    return lax.ppermute(array, axis, pairs)


def gelu_value(upper):
    inner = gelu_coef * (upper + 0.044715 * upper * upper * upper)
    return 0.5 * upper * (1.0 + jnp.tanh(inner))


def gelu_slope(upper):
    inner = gelu_coef * (upper + 0.044715 * upper * upper * upper)
    bent = jnp.tanh(inner)
    return 0.5 * (1.0 + bent) + 0.5 * upper * (1.0 - bent * bent) * gelu_coef * (
        1.0 + 3.0 * 0.044715 * upper * upper
    )


def normalize(inputs):
    values = inputs.astype(jnp.float32)
    center = jnp.mean(values, axis=-1, keepdims=True)
    spread = jnp.mean((values - center) * (values - center), axis=-1, keepdims=True)
    scaled = lax.rsqrt(spread + 1e-05)
    return ((values - center) * scaled, scaled)


def forward_block(inputs, first_matrix, second_matrix):
    normed, scaled = normalize(inputs)
    normed_b = normed.astype(jnp.bfloat16)
    upper = jnp.dot(normed_b, first_matrix, preferred_element_type=jnp.float32)
    hidden = gelu_value(upper).astype(jnp.bfloat16)
    mixed = lax.dot_general(
        hidden, second_matrix, (((1,), (1,)), ((), ())), preferred_element_type=jnp.float32
    )
    output = (inputs.astype(jnp.float32) + mixed).astype(jnp.bfloat16)
    return (output, normed, scaled, normed_b, upper, hidden)


def backward_block(grad_out, normed, scaled, upper, first_matrix, second_matrix):
    back_hidden = jnp.dot(grad_out, second_matrix, preferred_element_type=jnp.float32)
    back_upper = (back_hidden * gelu_slope(upper)).astype(jnp.bfloat16)
    back_normed = lax.dot_general(
        back_upper, first_matrix, (((1,), (1,)), ((), ())), preferred_element_type=jnp.float32
    )
    first_mean = jnp.mean(back_normed, axis=-1, keepdims=True)
    second_mean = jnp.mean(back_normed * normed, axis=-1, keepdims=True)
    grad_in = (
        grad_out.astype(jnp.float32) + scaled * (back_normed - first_mean - normed * second_mean)
    ).astype(jnp.bfloat16)
    return (grad_in, back_upper)


def row_product(left, right):
    return lax.dot_general(
        left, right, (((0,), (0,)), ((), ())), preferred_element_type=jnp.float32
    )


def local(token_ids, embed, weights, variance, momentum, worker_error, server_error, cotangent):
    section_count = lax.axis_size("section")
    section_index = lax.axis_index("section")
    replicas = lax.axis_size("dp")
    micro = token_ids.shape[0]
    rows = token_ids.shape[1]
    vocab = embed.shape[0]
    width = embed.shape[1]
    channels = weights.shape[3]
    owned = 2 * width // replicas
    shared = lax.all_gather(momentum[0], "dp", axis=0, tiled=True)
    first_matrix = weights[0, 0]
    second_matrix = weights[0, 1]
    one_hot = (token_ids[:, :, None] == lax.broadcasted_iota(jnp.int32, (1, 1, vocab), 2)).astype(
        jnp.bfloat16
    )
    embedded = jnp.einsum("mtv,vd->mtd", one_hot, embed, preferred_element_type=jnp.float32).astype(
        jnp.bfloat16
    )
    steps = micro + section_count - 1
    incoming = jnp.zeros((rows, width), jnp.bfloat16)
    saved_normed, saved_scaled, saved_bf, saved_upper, saved_hidden = ([], [], [], [], [])
    for step in range(steps):
        index = jnp.clip(step - section_index, 0, micro - 1)
        fresh = lax.dynamic_index_in_dim(embedded, index, 0, keepdims=False)
        inputs = jnp.where(section_index == 0, fresh, incoming)
        output, normed, scaled, normed_b, upper, hidden = forward_block(
            inputs, first_matrix, second_matrix
        )
        saved_normed.append(normed)
        saved_scaled.append(scaled)
        saved_bf.append(normed_b)
        saved_upper.append(upper)
        saved_hidden.append(hidden)
        if step + 1 < steps:
            incoming = passed_along(output, "section", 1)
    normed_all = jnp.stack(saved_normed)
    scaled_all = jnp.stack(saved_scaled)
    normed_bf_all = jnp.stack(saved_bf)
    upper_all = jnp.stack(saved_upper)
    hidden_all = jnp.stack(saved_hidden)
    grad_first = jnp.zeros((width, channels), jnp.float32)
    grad_second = jnp.zeros((width, channels), jnp.float32)
    back_in = jnp.zeros((rows, width), jnp.bfloat16)
    for step in range(steps):
        micro_index = step - (section_count - 1 - section_index)
        valid = jnp.logical_and(micro_index >= 0, micro_index < micro)
        clipped = jnp.clip(micro_index, 0, micro - 1)
        slot = jnp.clip(micro_index + section_index, 0, steps - 1)
        arriving = lax.dynamic_index_in_dim(cotangent, clipped, 0, keepdims=False)
        grad_out = jnp.where(section_index == section_count - 1, arriving, back_in)
        normed = lax.dynamic_index_in_dim(normed_all, slot, 0, keepdims=False)
        scaled = lax.dynamic_index_in_dim(scaled_all, slot, 0, keepdims=False)
        normed_b = lax.dynamic_index_in_dim(normed_bf_all, slot, 0, keepdims=False)
        upper = lax.dynamic_index_in_dim(upper_all, slot, 0, keepdims=False)
        hidden = lax.dynamic_index_in_dim(hidden_all, slot, 0, keepdims=False)
        grad_in, back_upper = backward_block(
            grad_out, normed, scaled, upper, first_matrix, second_matrix
        )
        grad_first = grad_first + jnp.where(valid, row_product(normed_b, back_upper), 0.0)
        grad_second = grad_second + jnp.where(valid, row_product(grad_out, hidden), 0.0)
        if step + 1 < steps:
            back_in = passed_along(grad_in, "section", -1)
    gradient = jnp.stack([grad_first, grad_second])
    combined = (
        0.9 * shared.astype(jnp.float32).reshape(2, width, channels)
        + 0.1 * gradient
        + worker_error[0, 0].astype(jnp.float32)
    )
    worker_scale = jnp.sqrt(jnp.mean(combined * combined) + 0.01)
    packed = (worker_scale * jnp.tanh(combined / worker_scale)).astype(jnp.bfloat16)
    new_worker = (combined - packed.astype(jnp.float32)).astype(jnp.bfloat16)[None, None]
    flat = packed.reshape(2 * width, channels)
    total = lax.psum_scatter(flat.astype(jnp.float32), "dp", scatter_dimension=0, tiled=True)
    merged = total / replicas + server_error[0]
    server_scale = jnp.sqrt(jnp.mean(merged * merged) + 0.01)
    server_values = (server_scale * jnp.tanh(merged / server_scale)).astype(jnp.bfloat16)
    new_server = (merged - server_values.astype(jnp.float32))[None]
    start = lax.axis_index("dp") * owned
    own_weights = lax.dynamic_slice_in_dim(weights[0].reshape(2 * width, channels), start, owned, 0)
    step_size = (
        0.01
        * server_values.astype(jnp.float32)
        / (jnp.sqrt(variance[0].astype(jnp.float32)) + 1e-08)
    )
    new_weights = (own_weights.astype(jnp.float32) - step_size).astype(jnp.bfloat16)[None]
    return (new_weights, server_values[None], new_worker, new_server)


def solution(mesh):
    in_specs = (
        P(None, "dp"),
        P(),
        P("section", None, None, None),
        P("section", "dp", None),
        P("section", "dp", None),
        P("section", "dp", None, None, None),
        P("section", "dp", None),
        P(None, "dp", None),
    )
    out_specs = (
        P("section", "dp", None),
        P("section", "dp", None),
        P("section", "dp", None, None, None),
        P("section", "dp", None),
    )
    return jax.shard_map(local, mesh=mesh, in_specs=in_specs, out_specs=out_specs, check_vma=False)
```

profile of v0, /device:TPU:0, one launch (start us, length us, event | category | flops | bytes accessed | tf_op | source)
XLA Modules:
  0.0 279.5 jit_solution(15378231506081991087)
XLA Ops:
  9.4 2.9 %bitcast_dynamic-update-slice_fusion.6 = (f32[7,64,2048]{2,1,0:T(8,128)}, f32[64,2048]{1,0:T(8,128)S(1)}) fusion(bf16[1,2,512,2048]{3,2,1,0:T(8,128)(2,1)} %param.10, f32[64]{0:T(128)S(1)} %add_rsqrt_fusion.6, f32[64]{0:T(128)S(1)} %broadcast_multiply_fusion.18, bf16[4,64,512]{2,1,0:T(8,128)(2,1)S(1)} %convolution_convert_fusion, s32[]{:T(128)S(6)} %min.64, ...), kind=kOutput, calls=%fused_computation.214 | convolution fusion | flops 134381568 | bytes 3212293 | tf_op jit(solution)/shard_map/dot_general | solution.py:41
  12.3 2.4 fusion.88
  14.6 4.9 %collective-permute-start = (bf16[64,512]{1,0:T(8,128)(2,1)S(1)}, bf16[64,512]{1,0:T(8,128)(2,1)S(1)}, u32[]{:S(2)}, u32[]{:S(2)}) collective-permute-start(bf16[64,512]{1,0:T(8,128)(2,1)S(1)} %fusion.88), channel_id=1, source_target_pairs={{0,8},{8,16},{16,24},{1,9},{9,17},{17,25},{2,10},{10,18},{18,26},{... | collective-permute-start | bytes 196616 | tf_op jit(solution)/shard_map/ppermute | solution.py:14
  22.5 3.1 %bitcast_dynamic-update-slice_fusion.5 = (f32[7,64,2048]{2,1,0:T(8,128)}, f32[64,2048]{1,0:T(8,128)S(1)}) fusion(f32[7,64,2048]{2,1,0:T(8,128)} %get-tuple-element.36, bf16[1,2,512,2048]{3,2,1,0:T(8,128)(2,1)} %param.10, bf16[64,512]{1,0:T(8,128)(2,1)S(1)} %get-tuple-element.29, f32[64]{0:T(128)S(1)} %add_rsqrt_fusion.5, f32[64]{0:T(128)S(1)} %broadcast_multiply_fusion.17), kind=kOutput, calls=%fused_computation.213 | convolution fusion | flops 134348800 | bytes 3211776 | tf_op jit(solution)/shard_map/dot_general | solution.py:41
  25.5 2.5 fusion.85
  28.0 4.3 %collective-permute-start.1 = (bf16[64,512]{1,0:T(8,128)(2,1)S(1)}, bf16[64,512]{1,0:T(8,128)(2,1)S(1)}, u32[]{:S(2)}, u32[]{:S(2)}) collective-permute-start(bf16[64,512]{1,0:T(8,128)(2,1)S(1)} %fusion.85), channel_id=1, source_target_pairs={{0,8},{8,16},{16,24},{1,9},{9,17},{17,25},{2,10},{10,18},{18,26},{... | collective-permute-start | bytes 196616 | tf_op jit(solution)/shard_map/ppermute | solution.py:14
  36.7 4.4 %collective-permute-start.2 = (bf16[64,512]{1,0:T(8,128)(2,1)S(1)}, bf16[64,512]{1,0:T(8,128)(2,1)S(1)}, u32[]{:S(2)}, u32[]{:S(2)}) collective-permute-start(bf16[64,512]{1,0:T(8,128)(2,1)S(1)} %fusion.82), channel_id=1, source_target_pairs={{0,8},{8,16},{16,24},{1,9},{9,17},{17,25},{2,10},{10,18},{18,26},{... | collective-permute-start | bytes 196616 | tf_op jit(solution)/shard_map/ppermute | solution.py:14
  44.7 5.2 %collective-permute-start.3 = (bf16[64,512]{1,0:T(8,128)(2,1)S(1)}, bf16[64,512]{1,0:T(8,128)(2,1)S(1)}, u32[]{:S(2)}, u32[]{:S(2)}) collective-permute-start(bf16[64,512]{1,0:T(8,128)(2,1)S(1)} %fusion.79), channel_id=1, source_target_pairs={{0,8},{8,16},{16,24},{1,9},{9,17},{17,25},{2,10},{10,18},{18,26},{... | collective-permute-start | bytes 196616 | tf_op jit(solution)/shard_map/ppermute | solution.py:14
  53.5 5.2 %collective-permute-start.4 = (bf16[64,512]{1,0:T(8,128)(2,1)S(1)}, bf16[64,512]{1,0:T(8,128)(2,1)S(1)}, u32[]{:S(2)}, u32[]{:S(2)}) collective-permute-start(bf16[64,512]{1,0:T(8,128)(2,1)S(1)} %fusion.76), channel_id=1, source_target_pairs={{0,8},{8,16},{16,24},{1,9},{9,17},{17,25},{2,10},{10,18},{18,26},{... | collective-permute-start | bytes 196616 | tf_op jit(solution)/shard_map/ppermute | solution.py:14
  62.3 5.2 %collective-permute-start.5 = (bf16[64,512]{1,0:T(8,128)(2,1)S(1)}, bf16[64,512]{1,0:T(8,128)(2,1)S(1)}, u32[]{:S(2)}, u32[]{:S(2)}) collective-permute-start(bf16[64,512]{1,0:T(8,128)(2,1)S(1)} %fusion.73), channel_id=1, source_target_pairs={{0,8},{8,16},{16,24},{1,9},{9,17},{17,25},{2,10},{10,18},{18,26},{... | collective-permute-start | bytes 196616 | tf_op jit(solution)/shard_map/ppermute | solution.py:14
  73.7 2.7 fusion.302
  77.3 2.2 collective-permute-done.6
  81.1 2.7 fusion.298
  86.0 5.4 %collective-permute-done.7 = bf16[64,512]{1,0:T(8,128)(2,1)S(1)} collective-permute-done((bf16[64,512]{1,0:T(8,128)(2,1)S(1)}, bf16[64,512]{1,0:T(8,128)(2,1)S(1)}, u32[]{:S(2)}, u32[]{:S(2)}) %collective-permute-start.7) | collective-permute-done | bytes 65568 | tf_op jit(solution)/shard_map/ppermute | solution.py:14
  93.0 2.7 fusion.296
  97.8 5.0 %collective-permute-done.8 = bf16[64,512]{1,0:T(8,128)(2,1)S(1)} collective-permute-done((bf16[64,512]{1,0:T(8,128)(2,1)S(1)}, bf16[64,512]{1,0:T(8,128)(2,1)S(1)}, u32[]{:S(2)}, u32[]{:S(2)}) %collective-permute-start.8) | collective-permute-done | bytes 65568 | tf_op jit(solution)/shard_map/ppermute | solution.py:14
  104.4 2.7 fusion.294
  109.3 5.0 %collective-permute-done.9 = bf16[64,512]{1,0:T(8,128)(2,1)S(1)} collective-permute-done((bf16[64,512]{1,0:T(8,128)(2,1)S(1)}, bf16[64,512]{1,0:T(8,128)(2,1)S(1)}, u32[]{:S(2)}, u32[]{:S(2)}) %collective-permute-start.9) | collective-permute-done | bytes 65568 | tf_op jit(solution)/shard_map/ppermute | solution.py:14
  117.3 2.7 fusion.292
  120.7 2.4 collective-permute-done.10
  126.3 2.7 fusion.290
  131.9 4.2 %select_add_fusion = f32[512,2048]{1,0:T(8,128)} fusion(f32[512,2048]{1,0:T(8,128)S(1)} %fusion.192, f32[512,2048]{1,0:T(8,128)S(1)} %fusion.194, f32[512,2048]{1,0:T(8,128)S(1)} %fusion.196, f32[512,2048]{1,0:T(8,128)S(1)} %fusion.198, f32[512,2048]{1,0:T(8,128)S(1)} %fusion.200, f32[512,2048]{1,0:T(8,128)S(1)} %fusion.202, pred[]{:T(512)S(6)} %and.29, ...), kind=kOutput, calls=%fused_computation.12 | convolution fusion | flops 147881984 | bytes 29753360 | tf_op jit(solution)/shard_map/dot_general | solution.py:65
  136.0 9.9 %select_add_fusion.1 = f32[512,2048]{1,0:T(8,128)} fusion(f32[512,2048]{1,0:T(8,128)} %fusion.290, f32[512,2048]{1,0:T(8,128)} %fusion.292, f32[512,2048]{1,0:T(8,128)} %fusion.294, f32[512,2048]{1,0:T(8,128)} %fusion.296, f32[512,2048]{1,0:T(8,128)} %fusion.298, f32[512,2048]{1,0:T(8,128)} %fusion.302, pred[]{:T(512)S(6)} %and.29, pred[]{:T(512)S(6)} %and.28, ...), kind=kOutput, calls=%fused_computation.13 | convolution fusion | flops 284590080 | bytes 32183808 | tf_op jit(solution)/shard_map/dot_general | solution.py:65
  145.9 8.5 %maximum_multiply_fusion = f32[2,512,2048]{2,1,0:T(8,128)} fusion(f32[1,512,2048]{2,1,0:T(8,128)} %bitcast.529, f32[1,512,2048]{2,1,0:T(8,128)} %bitcast.531), kind=kLoop, calls=%fused_computation | loop fusion | flops 4194304 | bytes 16777216 | tf_op jit(solution)/shard_map/mul | solution.py:136
  154.4 7.6 %multiply_reduce_fusion = f32[]{:T(128)} fusion(bf16[1,1,2,512,2048]{4,3,2,1,0:T(8,128)(2,1)} %param.13, f32[2,512,2048]{2,1,0:T(8,128)} %maximum_multiply_fusion, bf16[1,1024,2048]{2,1,0:T(8,128)(2,1)} %all-gather.3.cloned.1.call-done), kind=kLoop, calls=%fused_computation.10 | loop fusion | flops 14680063 | bytes 16777220 | tf_op jit(solution)/shard_map/reduce_sum | solution.py:139
  162.7 9.4 %fusion.2 = f32[1024,2048]{1,0:T(8,128)} fusion(f32[]{:T(128)S(6)} %sqrt.10, bf16[1,1,2,512,2048]{4,3,2,1,0:T(8,128)(2,1)} %param.13, f32[2,512,2048]{2,1,0:T(8,128)} %maximum_multiply_fusion, bf16[1,1024,2048]{2,1,0:T(8,128)(2,1)} %all-gather.3.cloned.1.call-done), kind=kLoop, calls=%fused_computation.11 | loop fusion | flops 18874368 | bytes 25165828 | tf_op jit(solution)/shard_map/convert_element_type | solution.py:143
  172.2 3.5 %convert_multiply_fusion = f32[1,1024,2048]{2,1,0:T(8,128)S(1)} fusion(bf16[1,1024,2048]{2,1,0:T(8,128)(2,1)} %all-gather.3.cloned.1.call-done), kind=kLoop, calls=%fused_computation.6 | loop fusion | flops 4194304 | bytes 12582912 | tf_op jit(solution)/shard_map/mul | solution.py:135
  178.1 4.1 %subtract_convert_fusion = bf16[1,1,2,512,2048]{4,3,2,1,0:T(8,128)(2,1)} fusion(f32[1,1,2,512,2048]{4,3,2,1,0:T(8,128)S(1)} %bitcast.533, f32[1,1,1,512,2048]{4,3,2,1,0:T(8,128)S(1)} %bitcast.530, f32[1,1,1,512,2048]{4,3,2,1,0:T(8,128)S(1)} %bitcast.532, f32[]{:T(128)S(6)} %sqrt.10, bf16[1,1,2,512,2048]{4,3,2,1,0:T(8,128)(2,1)S(1)} %copy-done.3), kind=kLoop, calls=%fused_computation.7 | loop fusion | flops 23068672 | bytes 25165828 | tf_op jit(solution)/shard_map/convert_element_type | solution.py:141
  182.1 82.7 %reduce-scatter.2.cloned.1.call-done = f32[128,2048]{1,0:T(8,128)} async-done(((f32[1024,2048]{1,0:T(8,128)}), f32[128,2048]{1,0:T(8,128)}) %reduce-scatter.2.cloned.1.call-update) | async-done | bytes 1048592 | tf_op jit(solution)/shard_map/reduce_scatter | solution.py:143
  264.8 2.1 multiply_reduce_fusion.1
  267.6 2.4 fusion.94
  270.1 2.6 fusion.190
  (157 shorter events, 50.2 us)
Async XLA Ops:
  7.2 0.9 copy-start
  7.2 147.2 %all-gather.3.cloned.1.call-start = ((), (), s32[]{:S(2)}) async-start(), calls=%async_computation.2 | async-start | bytes 4718592 | tf_op jit(solution)/shard_map/all_gather | solution.py:80
  14.6 6.8 %collective-permute-start = (bf16[64,512]{1,0:T(8,128)(2,1)S(1)}, bf16[64,512]{1,0:T(8,128)(2,1)S(1)}, u32[]{:S(2)}, u32[]{:S(2)}) collective-permute-start(bf16[64,512]{1,0:T(8,128)(2,1)S(1)} %fusion.88), channel_id=1, source_target_pairs={{0,8},{8,16},{16,24},{1,9},{9,17},{17,25},{2,10},{10,18},{18,26},{... | collective-permute-start | bytes 196616 | tf_op jit(solution)/shard_map/ppermute | solution.py:14
  19.5 245.3 %reduce-scatter.2.cloned.1.call-start = ((), (), s32[]{:S(2)}) async-start(), calls=%async_computation.1 | async-start | bytes 9437184 | tf_op jit(solution)/shard_map/reduce_scatter | solution.py:143
  22.5 12.0 %copy-start.9 = (f32[7,64,512]{2,1,0:T(8,128)S(1)}, f32[7,64,512]{2,1,0:T(8,128)}, u32[]{:S(2)}) copy-start(f32[7,64,512]{2,1,0:T(8,128)} %fusion.242) | copy-start | bytes 2752516
  22.5 12.1 %copy-start.2 = (bf16[1,2,512,2048]{3,2,1,0:T(8,128)(2,1)S(1)}, bf16[1,2,512,2048]{3,2,1,0:T(8,128)(2,1)}, u32[]{:S(2)}) copy-start(bf16[1,2,512,2048]{3,2,1,0:T(8,128)(2,1)} %param.10) | copy-start | bytes 12582916
  28.0 6.2 %collective-permute-start.1 = (bf16[64,512]{1,0:T(8,128)(2,1)S(1)}, bf16[64,512]{1,0:T(8,128)(2,1)S(1)}, u32[]{:S(2)}, u32[]{:S(2)}) collective-permute-start(bf16[64,512]{1,0:T(8,128)(2,1)S(1)} %fusion.85), channel_id=1, source_target_pairs={{0,8},{8,16},{16,24},{1,9},{9,17},{17,25},{2,10},{10,18},{18,26},{... | collective-permute-start | bytes 196616 | tf_op jit(solution)/shard_map/ppermute | solution.py:14
  35.9 7.5 %copy-start.14 = (f32[7,64,2048]{2,1,0:T(8,128)S(1)}, f32[7,64,2048]{2,1,0:T(8,128)}, u32[]{:S(2)}) copy-start(f32[7,64,2048]{2,1,0:T(8,128)} %get-tuple-element.40) | copy-start | bytes 11010052
  36.7 6.3 %collective-permute-start.2 = (bf16[64,512]{1,0:T(8,128)(2,1)S(1)}, bf16[64,512]{1,0:T(8,128)(2,1)S(1)}, u32[]{:S(2)}, u32[]{:S(2)}) collective-permute-start(bf16[64,512]{1,0:T(8,128)(2,1)S(1)} %fusion.82), channel_id=1, source_target_pairs={{0,8},{8,16},{16,24},{1,9},{9,17},{17,25},{2,10},{10,18},{18,26},{... | collective-permute-start | bytes 196616 | tf_op jit(solution)/shard_map/ppermute | solution.py:14
  44.7 7.1 %collective-permute-start.3 = (bf16[64,512]{1,0:T(8,128)(2,1)S(1)}, bf16[64,512]{1,0:T(8,128)(2,1)S(1)}, u32[]{:S(2)}, u32[]{:S(2)}) collective-permute-start(bf16[64,512]{1,0:T(8,128)(2,1)S(1)} %fusion.79), channel_id=1, source_target_pairs={{0,8},{8,16},{16,24},{1,9},{9,17},{17,25},{2,10},{10,18},{18,26},{... | collective-permute-start | bytes 196616 | tf_op jit(solution)/shard_map/ppermute | solution.py:14
  53.5 7.1 %collective-permute-start.4 = (bf16[64,512]{1,0:T(8,128)(2,1)S(1)}, bf16[64,512]{1,0:T(8,128)(2,1)S(1)}, u32[]{:S(2)}, u32[]{:S(2)}) collective-permute-start(bf16[64,512]{1,0:T(8,128)(2,1)S(1)} %fusion.76), channel_id=1, source_target_pairs={{0,8},{8,16},{16,24},{1,9},{9,17},{17,25},{2,10},{10,18},{18,26},{... | collective-permute-start | bytes 196616 | tf_op jit(solution)/shard_map/ppermute | solution.py:14
  59.0 2.0 copy-start.10
  61.6 6.1 %copy-start.11 = (bf16[7,64,512]{2,1,0:T(8,128)(2,1)S(1)}, bf16[7,64,512]{2,1,0:T(8,128)(2,1)}, u32[]{:S(2)}) copy-start(bf16[7,64,512]{2,1,0:T(8,128)(2,1)} %copy-done.10) | copy-start | bytes 1376260
  61.6 8.8 %copy-start.8 = (bf16[4,64,512]{2,1,0:T(8,128)(2,1)S(1)}, bf16[4,64,512]{2,1,0:T(8,128)(2,1)}, u32[]{:S(2)}) copy-start(bf16[4,64,512]{2,1,0:T(8,128)(2,1)} %param.15) | copy-start | bytes 786436
  62.3 7.1 %collective-permute-start.5 = (bf16[64,512]{1,0:T(8,128)(2,1)S(1)}, bf16[64,512]{1,0:T(8,128)(2,1)S(1)}, u32[]{:S(2)}, u32[]{:S(2)}) collective-permute-start(bf16[64,512]{1,0:T(8,128)(2,1)S(1)} %fusion.73), channel_id=1, source_target_pairs={{0,8},{8,16},{16,24},{1,9},{9,17},{17,25},{2,10},{10,18},{18,26},{... | collective-permute-start | bytes 196616 | tf_op jit(solution)/shard_map/ppermute | solution.py:14
  70.4 52.7 %copy-start.15 = (f32[7,64,2048]{2,1,0:T(8,128)}, f32[7,64,2048]{2,1,0:T(8,128)S(1)}, u32[]{:S(2)}) copy-start(f32[7,64,2048]{2,1,0:T(8,128)S(1)} %get-tuple-element.48) | copy-start | bytes 11010052
  72.1 7.4 %collective-permute-start.6 = (bf16[64,512]{1,0:T(8,128)(2,1)S(1)}, bf16[64,512]{1,0:T(8,128)(2,1)S(1)}, u32[]{:S(2)}, u32[]{:S(2)}) collective-permute-start(bf16[64,512]{1,0:T(8,128)(2,1)S(1)} %fusion.287), channel_id=1, source_target_pairs={{8,0},{16,8},{24,16},{9,1},{17,9},{25,17},{10,2},{18,10},{26,18},{... | collective-permute-start | bytes 196616 | tf_op jit(solution)/shard_map/ppermute | solution.py:14
  73.7 52.6 %copy-start.12 = (bf16[7,64,512]{2,1,0:T(8,128)(2,1)}, bf16[7,64,512]{2,1,0:T(8,128)(2,1)S(1)}, u32[]{:S(2)}) copy-start(bf16[7,64,512]{2,1,0:T(8,128)(2,1)S(1)} %constant_dynamic-update-slice_fusion) | copy-start | bytes 1376260
  83.9 7.4 %collective-permute-start.7 = (bf16[64,512]{1,0:T(8,128)(2,1)S(1)}, bf16[64,512]{1,0:T(8,128)(2,1)S(1)}, u32[]{:S(2)}, u32[]{:S(2)}) collective-permute-start(bf16[64,512]{1,0:T(8,128)(2,1)S(1)} %fusion.282), channel_id=1, source_target_pairs={{8,0},{16,8},{24,16},{9,1},{17,9},{25,17},{10,2},{18,10},{26,18},{... | collective-permute-start | bytes 196616 | tf_op jit(solution)/shard_map/ppermute | solution.py:14
  95.8 7.1 %collective-permute-start.8 = (bf16[64,512]{1,0:T(8,128)(2,1)S(1)}, bf16[64,512]{1,0:T(8,128)(2,1)S(1)}, u32[]{:S(2)}, u32[]{:S(2)}) collective-permute-start(bf16[64,512]{1,0:T(8,128)(2,1)S(1)} %fusion.277), channel_id=1, source_target_pairs={{8,0},{16,8},{24,16},{9,1},{17,9},{25,17},{10,2},{18,10},{26,18},{... | collective-permute-start | bytes 196616 | tf_op jit(solution)/shard_map/ppermute | solution.py:14
  107.3 7.1 %collective-permute-start.9 = (bf16[64,512]{1,0:T(8,128)(2,1)S(1)}, bf16[64,512]{1,0:T(8,128)(2,1)S(1)}, u32[]{:S(2)}, u32[]{:S(2)}) collective-permute-start(bf16[64,512]{1,0:T(8,128)(2,1)S(1)} %fusion.272), channel_id=1, source_target_pairs={{8,0},{16,8},{24,16},{9,1},{17,9},{25,17},{10,2},{18,10},{26,18},{... | collective-permute-start | bytes 196616 | tf_op jit(solution)/shard_map/ppermute | solution.py:14
  116.0 7.1 %collective-permute-start.10 = (bf16[64,512]{1,0:T(8,128)(2,1)S(1)}, bf16[64,512]{1,0:T(8,128)(2,1)S(1)}, u32[]{:S(2)}, u32[]{:S(2)}) collective-permute-start(bf16[64,512]{1,0:T(8,128)(2,1)S(1)} %fusion.267), channel_id=1, source_target_pairs={{8,0},{16,8},{24,16},{9,1},{17,9},{25,17},{10,2},{18,10},{26,18},{... | collective-permute-start | bytes 196616 | tf_op jit(solution)/shard_map/ppermute | solution.py:14
  124.8 7.1 %collective-permute-start.11 = (bf16[64,512]{1,0:T(8,128)(2,1)S(1)}, bf16[64,512]{1,0:T(8,128)(2,1)S(1)}, u32[]{:S(2)}, u32[]{:S(2)}) collective-permute-start(bf16[64,512]{1,0:T(8,128)(2,1)S(1)} %fusion.262), channel_id=1, source_target_pairs={{8,0},{16,8},{24,16},{9,1},{17,9},{25,17},{10,2},{18,10},{26,18},{... | collective-permute-start | bytes 196616 | tf_op jit(solution)/shard_map/ppermute | solution.py:14
  172.1 3.6 %copy-start.3 = (bf16[1,1,2,512,2048]{4,3,2,1,0:T(8,128)(2,1)S(1)}, bf16[1,1,2,512,2048]{4,3,2,1,0:T(8,128)(2,1)}, u32[]{:S(2)}) copy-start(bf16[1,1,2,512,2048]{4,3,2,1,0:T(8,128)(2,1)} %param.13) | copy-start | bytes 12582916
  172.1 4.7 %copy-start.4 = (f32[512,2048]{1,0:T(8,128)S(1)}, f32[512,2048]{1,0:T(8,128)}, u32[]{:S(2)}) copy-start(f32[512,2048]{1,0:T(8,128)} %select_add_fusion) | copy-start | bytes 12582916
  172.2 5.9 %copy-start.5 = (f32[512,2048]{1,0:T(8,128)S(1)}, f32[512,2048]{1,0:T(8,128)}, u32[]{:S(2)}) copy-start(f32[512,2048]{1,0:T(8,128)} %select_add_fusion.1) | copy-start | bytes 12582916
  178.1 86.8 %copy-start.6 = (f32[1,128,2048]{2,1,0:T(8,128)S(1)}, f32[1,128,2048]{2,1,0:T(8,128)}, u32[]{:S(2)}) copy-start(f32[1,128,2048]{2,1,0:T(8,128)} %param.14) | copy-start | bytes 3145732
  178.1 94.6 %copy-start.1 = (bf16[128,512]{1,0:T(8,128)(2,1)S(1)}, bf16[128,512]{1,0:T(8,128)(2,1)}, u32[]{:S(2)}) copy-start(bf16[128,512]{1,0:T(8,128)(2,1)} %param.9) | copy-start | bytes 393220
  182.1 87.9 %copy-start.13 = (bf16[1,128,2048]{2,1,0:T(8,128)(2,1)S(1)}, bf16[1,128,2048]{2,1,0:T(8,128)(2,1)}, u32[]{:S(2)}) copy-start(bf16[1,128,2048]{2,1,0:T(8,128)(2,1)} %param.11) | copy-start | bytes 1572868
  270.1 2.6 copy-start.7
Sparse Core Ops, SparseCore 0:
  19.7 47.1 all-gather.2
  172.3 92.5 reduce-scatter.1
where the time goes:
time: 280 us; the launch traced here: 279 us
  waiting for transfers between devices  114 us (41%)
  matrix products  62.2 us (22%)
  other arithmetic  46.9 us (17%)
  starting transfers between devices  37.3 us (13%)
  between operations  16.3 us (6%)
  local copies, waits for them, and re-layouts  3.27 us (1%)
    reduce_scatter x1, waiting for transfers between devices, local(): lax.psum_scatter(flat.astype(jnp.float32), 'dp', scatter_dimension=0, til...  82.7 us
    ppermute x12, starting transfers between devices, passed_along(): return lax.ppermute(array, axis, pairs)  37.2 us
    dot_general x14, matrix products, row_product(): lax.dot_general(left, right, (((0,), (0,)), ((), ())), preferred_element_...  34.6 us
    ppermute x12, waiting for transfers between devices, passed_along(): return lax.ppermute(array, axis, pairs)  30.8 us
    dot_general x7, matrix products, forward_block(): upper = jnp.dot(normed_b, first_matrix, preferred_element_type=jnp.float32)  9.4 us
    convert_element_type x1, other arithmetic, local(): flat.astype(jnp.float32)  9.37 us
    mul x1, other arithmetic, local(): 0.1 * gradient  8.49 us
    dot_general x6, matrix products, forward_block(): lax.dot_general(hidden, second_matrix, (((1,), (1,)), ((), ())), preferre...  7.88 us
  transfers between devices with their start and end apart: 14, of which 13 were waited for; matrix products, arithmetic and copies ran while one was open for 28% of the time, Pallas kernels for 0%

commit v1 on v0

v1 whole, which is shorter than its diff:
```python
import functools
import math

import jax
import jax.numpy as jnp
from jax import lax
from jax.experimental import pallas as pl
from jax.experimental.pallas import tpu as pltpu
from jax.sharding import PartitionSpec as P

gelu_coef = math.sqrt(2.0 / math.pi)
MESH = pl.DeviceIdType.MESH
NT = (((1,), (1,)), ((), ()))
TN = (((0,), (0,)), ((), ()))


def dot(left, right, dims=(((1,), (0,)), ((), ()))):
    return lax.dot_general(left, right, dims, preferred_element_type=jnp.float32)


def dp_device(index):
    return {"section": lax.axis_index("section"), "dp": index}


def section_device(index):
    return {"section": index, "dp": lax.axis_index("dp")}


def signal(semaphore, device):
    pl.semaphore_signal(semaphore, inc=1, device_id=device, device_id_type=MESH)


def remote(src, dst, send, recv, device):
    return pltpu.make_async_remote_copy(
        src_ref=src, dst_ref=dst, send_sem=send, recv_sem=recv, device_id=device, device_id_type=MESH
    )


def block_kernel(
    sections, chips, ids, embed, weights, cotangent, momentum, left, right, shared,
    arrived, outgoing, back_arrived, back_outgoing, normed_s, scaled_s, slope_s,
    fwd_send, fwd_recv, bwd_send, bwd_recv, own_sem, far_send, far_recv, pair_send, pair_recv,
):
    micro, rows, width = cotangent.shape
    vocab = embed.shape[0]
    channels = weights.shape[-1]
    tile = min(512, channels)
    owned = momentum.shape[0]
    section = lax.axis_index("section")
    me = lax.axis_index("dp")
    chip, core = me // 2, me % 2
    partner = chip * 2 + 1 - core
    first, last = section == 0, section == sections - 1
    ahead, behind = lax.rem(section + 1, sections), lax.rem(section + sections - 1, sections)

    barrier = pltpu.get_barrier_semaphore()
    signal(barrier, section_device(ahead))
    signal(barrier, section_device(behind))
    signal(barrier, dp_device(partner))
    for j in range(1, chips):
        signal(barrier, dp_device(lax.rem(chip + j, chips) * 2 + core))
    pl.semaphore_wait(barrier, 2 + chips)

    def span(index):
        return pl.ds(pl.multiple_of(index * owned, owned), owned)

    own_copy = pltpu.make_async_copy(momentum, shared.at[span(me)], own_sem)
    own_copy.start()
    far = []
    for j in range(1, chips):
        target = lax.rem(chip + j, chips) * 2 + core
        far.append(remote(momentum, shared.at[span(me)], far_send.at[j], far_recv.at[j], dp_device(target)))
        far[-1].start()
    pair = [remote(momentum, shared.at[span(me)], pair_send.at[0], pair_recv.at[0], dp_device(partner))]
    pair[0].start()

    def fwd_copy(m):
        return remote(outgoing.at[m], arrived.at[m], fwd_send.at[m], fwd_recv.at[m], section_device(ahead))

    def bwd_copy(m):
        return remote(
            back_outgoing.at[m], back_arrived.at[m], bwd_send.at[m], bwd_recv.at[m], section_device(behind)
        )

    @pl.when(first)
    def _():
        for m in range(micro):
            hot = ids[m : m + 1, :] == lax.broadcasted_iota(jnp.int32, (vocab, rows), 0)
            hot = jnp.where(hot, 1.0, 0.0).astype(jnp.bfloat16)
            arrived[m] = dot(hot, embed[...], TN).astype(jnp.bfloat16)

    def forward(m, carry):
        @pl.when(jnp.logical_not(first))
        def _():
            fwd_copy(m).wait_recv()

        values = arrived[m].astype(jnp.float32)
        center = jnp.mean(values, axis=-1, keepdims=True)
        shifted = values - center
        spread = jnp.mean(shifted * shifted, axis=-1, keepdims=True)
        scaled = lax.rsqrt(spread + 1e-05)
        normed = shifted * scaled
        normed_b = normed.astype(jnp.bfloat16)
        normed_s[m] = normed
        scaled_s[m] = scaled
        left[0, m] = normed_b
        mixed = values
        for start in range(0, channels, tile):
            cut = slice(start, start + tile)
            upper = dot(normed_b, weights[0, 0, :, cut])
            square = upper * upper
            bent = jnp.tanh(gelu_coef * (upper + 0.044715 * upper * square))
            half = 0.5 * (1.0 + bent)
            hidden = (upper * half).astype(jnp.bfloat16)
            right[1, m, :, cut] = hidden
            slope_s[m, :, cut] = half + 0.5 * upper * (1.0 - bent * bent) * gelu_coef * (
                1.0 + 3.0 * 0.044715 * square
            )
            mixed = mixed + dot(hidden, weights[0, 1, :, cut], NT)
        outgoing[m] = mixed.astype(jnp.bfloat16)

        @pl.when(jnp.logical_not(last))
        def _():
            fwd_copy(m).start()

        return carry

    lax.fori_loop(0, micro, forward, 0)

    def backward(m, carry):
        @pl.when(last)
        def _():
            left[1, m] = cotangent[m]

        @pl.when(jnp.logical_not(last))
        def _():
            bwd_copy(m).wait_recv()
            left[1, m] = back_arrived[m]

        grad_out = left[1, m]
        back_normed = jnp.zeros((rows, width), jnp.float32)
        for start in range(0, channels, tile):
            cut = slice(start, start + tile)
            back_hidden = dot(grad_out, weights[0, 1, :, cut])
            back_upper = (back_hidden * slope_s[m, :, cut]).astype(jnp.bfloat16)
            right[0, m, :, cut] = back_upper
            back_normed = back_normed + dot(back_upper, weights[0, 0, :, cut], NT)

        @pl.when(jnp.logical_not(first))
        def _():
            normed = normed_s[m]
            first_mean = jnp.mean(back_normed, axis=-1, keepdims=True)
            second_mean = jnp.mean(back_normed * normed, axis=-1, keepdims=True)
            back_outgoing[m] = (
                grad_out.astype(jnp.float32) + scaled_s[m] * (back_normed - first_mean - normed * second_mean)
            ).astype(jnp.bfloat16)
            bwd_copy(m).start()

        return carry

    lax.fori_loop(0, micro, backward, 0)

    own_copy.wait()
    for j in range(1, chips):
        far[j - 1].wait()
        origin = span(lax.rem(chip + chips - j, chips) * 2 + core)
        pair.append(
            remote(shared.at[origin], shared.at[origin], pair_send.at[j], pair_recv.at[j], dp_device(partner))
        )
        pair[-1].start()
    for copy in pair:
        copy.wait()

    @pl.when(jnp.logical_not(last))
    def _():
        for m in range(micro):
            fwd_copy(m).wait_send()

    @pl.when(jnp.logical_not(first))
    def _():
        for m in range(micro):
            bwd_copy(m).wait_send()


def run_blocks(sections, chips, ids, embed, weights, cotangent, momentum):
    micro, rows, width = cotangent.shape
    channels = weights.shape[-1]
    vmem = pl.BlockSpec(memory_space=pltpu.VMEM)
    hbm = pl.BlockSpec(memory_space=pl.ANY)
    relay = pltpu.VMEM((micro, rows, width), jnp.bfloat16)
    dma = pltpu.SemaphoreType.DMA
    return pl.pallas_call(
        functools.partial(block_kernel, sections, chips),
        out_shape=(
            jax.ShapeDtypeStruct((2, micro, rows, width), jnp.bfloat16),
            jax.ShapeDtypeStruct((2, micro, rows, channels), jnp.bfloat16),
            jax.ShapeDtypeStruct((2 * width, channels), jnp.bfloat16),
        ),
        in_specs=[vmem, vmem, vmem, vmem, hbm],
        out_specs=(vmem, vmem, hbm),
        scratch_shapes=[
            relay, relay, relay, relay,
            pltpu.VMEM((micro, rows, width), jnp.float32),
            pltpu.VMEM((micro, rows, 1), jnp.float32),
            pltpu.VMEM((micro, rows, channels), jnp.float32),
            dma((micro,)), dma((micro,)), dma((micro,)), dma((micro,)),
            dma, dma((chips,)), dma((chips,)), dma((chips,)), dma((chips,)),
        ],
        compiler_params=pltpu.CompilerParams(
            collective_id=0, has_side_effects=True, vmem_limit_bytes=48 * 1024 * 1024
        ),
        name="blocks",
    )(ids, embed, weights, cotangent, momentum)


def pack_kernel(count, left, right, shared, error, packed, fresh, combined, total):
    phase, step = pl.program_id(0), pl.program_id(1)

    @pl.when(jnp.logical_and(phase == 0, step == 0))
    def _():
        total[...] = jnp.zeros_like(total)

    @pl.when(phase == 0)
    def _():
        gradient = dot(left[0], right[0], TN)
        values = 0.9 * shared[...].astype(jnp.float32) + 0.1 * gradient + error[...].astype(jnp.float32)
        combined[step] = values
        total[...] += jnp.sum(values * values, axis=0, keepdims=True)

    @pl.when(phase == 1)
    def _():
        mean = jnp.sum(total[...], axis=1, keepdims=True) / count
        scale = jnp.sqrt(mean + 0.01)
        values = combined[step]
        narrow = (scale * jnp.tanh(values * (1.0 / scale))).astype(jnp.bfloat16)
        packed[...] = narrow
        fresh[...] = (values - narrow.astype(jnp.float32)).astype(jnp.bfloat16)


def pack(left, right, shared, error):
    _, tokens, width = left.shape
    channels = right.shape[-1]
    tile = 128
    per = width // tile
    steps = 2 * per

    def when_first(phase, step):
        return jnp.where(phase == 0, step, steps - 1)

    rows_in = pl.BlockSpec((tile, channels), lambda p, i: (when_first(p, i), 0))
    rows_out = pl.BlockSpec((tile, channels), lambda p, i: (jnp.where(p == 0, 0, i), 0))
    out = jax.ShapeDtypeStruct((2 * width, channels), jnp.bfloat16)
    return pl.pallas_call(
        functools.partial(pack_kernel, float(2 * width * channels)),
        grid=(2, steps),
        out_shape=(out, out),
        in_specs=[
            pl.BlockSpec((1, tokens, tile), lambda p, i: (when_first(p, i) // per, 0, when_first(p, i) % per)),
            pl.BlockSpec((1, tokens, channels), lambda p, i: (when_first(p, i) // per, 0, 0)),
            rows_in,
            rows_in,
        ],
        out_specs=(rows_out, rows_out),
        scratch_shapes=[
            pltpu.VMEM((steps, tile, channels), jnp.float32),
            pltpu.VMEM((1, channels), jnp.float32),
        ],
        compiler_params=pltpu.CompilerParams(
            dimension_semantics=("arbitrary", "arbitrary"), vmem_limit_bytes=48 * 1024 * 1024
        ),
        name="pack",
    )(left, right, shared, error)


def merge_kernel(
    chips, packed, total, own, paired, outgoing, arrived,
    own_sem, pair_send, pair_recv, far_send, far_recv,
):
    owned = total.shape[0]
    me = lax.axis_index("dp")
    chip, core = me // 2, me % 2
    other = 1 - core
    partner = chip * 2 + other

    barrier = pltpu.get_barrier_semaphore()
    signal(barrier, dp_device(partner))
    for j in range(1, chips):
        signal(barrier, dp_device(lax.rem(chip + j, chips) * 2 + core))
    pl.semaphore_wait(barrier, chips)

    def span(index):
        return pl.ds(pl.multiple_of(index * owned, owned), owned)

    order = list(range(1, chips)) + [0]
    local, pair, far = {}, {}, {}
    for j in order:
        target = lax.rem(chip + j, chips) * 2
        pair[j] = remote(
            packed.at[span(target + other)], paired.at[j], pair_send.at[j], pair_recv.at[j], dp_device(partner)
        )
        pair[j].start()
        local[j] = pltpu.make_async_copy(packed.at[span(target + core)], own.at[j], own_sem.at[j])
        local[j].start()
    for j in order:
        local[j].wait()
        pair[j].wait()
        both = own[j].astype(jnp.float32) + paired[j].astype(jnp.float32)
        if j == 0:
            total[...] = both
        else:
            outgoing[j - 1] = both.astype(jnp.bfloat16)
            target = lax.rem(chip + j, chips) * 2 + core
            far[j] = remote(
                outgoing.at[j - 1], arrived.at[j - 1], far_send.at[j], far_recv.at[j], dp_device(target)
            )
            far[j].start()
    for j in range(1, chips):
        far[j].wait()
        total[...] += arrived[j - 1].astype(jnp.float32)


def merge(chips, packed):
    rows, channels = packed.shape
    owned = rows // (2 * chips)
    dma = pltpu.SemaphoreType.DMA
    return pl.pallas_call(
        functools.partial(merge_kernel, chips),
        out_shape=jax.ShapeDtypeStruct((owned, channels), jnp.float32),
        in_specs=[pl.BlockSpec(memory_space=pl.ANY)],
        out_specs=pl.BlockSpec(memory_space=pltpu.VMEM),
        scratch_shapes=[
            pltpu.VMEM((chips, owned, channels), jnp.bfloat16),
            pltpu.VMEM((chips, owned, channels), jnp.bfloat16),
            pltpu.VMEM((chips - 1, owned, channels), jnp.bfloat16),
            pltpu.VMEM((chips - 1, owned, channels), jnp.bfloat16),
            dma((chips,)), dma((chips,)), dma((chips,)), dma((chips,)), dma((chips,)),
        ],
        compiler_params=pltpu.CompilerParams(
            collective_id=1, has_side_effects=True, vmem_limit_bytes=48 * 1024 * 1024
        ),
        name="merge",
    )(packed)


def local(sections, replicas, token_ids, embed, weights, variance, momentum, worker_error, server_error, cotangent):
    width, channels = weights.shape[2:]
    owned = 2 * width // replicas
    chips = replicas // 2
    left, right, shared = run_blocks(sections, chips, token_ids, embed, weights, cotangent, momentum[0])
    packed, new_worker = pack(
        left.reshape(2, -1, width),
        right.reshape(2, -1, channels),
        shared,
        worker_error.reshape(2 * width, channels),
    )
    total = merge(chips, packed)
    merged = total / replicas + server_error[0]
    server_scale = jnp.sqrt(jnp.mean(merged * merged) + 0.01)
    server_values = (server_scale * jnp.tanh(merged / server_scale)).astype(jnp.bfloat16)
    new_server = (merged - server_values.astype(jnp.float32))[None]
    start = lax.axis_index("dp") * owned
    own_weights = lax.dynamic_slice_in_dim(weights[0].reshape(2 * width, channels), start, owned, 0)
    step_size = (
        0.01 * server_values.astype(jnp.float32) / (jnp.sqrt(variance[0].astype(jnp.float32)) + 1e-08)
    )
    new_weights = (own_weights.astype(jnp.float32) - step_size).astype(jnp.bfloat16)[None]
    return (new_weights, server_values[None], new_worker.reshape(worker_error.shape), new_server)


def solution(mesh):
    in_specs = (
        P(None, "dp"),
        P(),
        P("section", None, None, None),
        P("section", "dp", None),
        P("section", "dp", None),
        P("section", "dp", None, None, None),
        P("section", "dp", None),
        P(None, "dp", None),
    )
    out_specs = (
        P("section", "dp", None),
        P("section", "dp", None),
        P("section", "dp", None, None, None),
        P("section", "dp", None),
    )
    body = functools.partial(local, mesh.shape["section"], mesh.shape["dp"])
    return jax.shard_map(body, mesh=mesh, in_specs=in_specs, out_specs=out_specs, check_vma=False)
```

time: 280 us -> 132 us (0.47)
  the two profiles are of different devices: /device:TPU:0 before, /device:TPU:9 now
where the time goes in v1:
time: 132 us; the launch traced here: 131 us
  Pallas kernels  119 us (90%)
  local copies, waits for them, and re-layouts  5.77 us (4%)
  other arithmetic  4.64 us (4%)
  between operations  1.37 us (1%)
    pallas_call x1, Pallas kernels, run_blocks(): pl.pallas_call(functools.partial(block_kernel, sections, chips), out_shap...  54.4 us
    pallas_call x1, Pallas kernels, merge(): pl.pallas_call(functools.partial(merge_kernel, chips), out_shape=jax.Shap...  50.8 us
    pallas_call x1, Pallas kernels, pack(): pl.pallas_call(functools.partial(pack_kernel, float(2 * width * channels)...  14.1 us
    unnamed x16, local copies, waits for them, and re-layouts  5.77 us

profile of v1, /device:TPU:9, one launch (start us, length us, event | category | flops | bytes accessed | tf_op | source)
XLA Modules:
  0.0 131.1 jit_solution(3028893739303743255)
XLA Ops:
  0.6 0.0 copy-start.1
  0.6 1.0 copy-done.1
  1.7 0.0 copy-start.2
  1.7 0.9 copy-done.2
  2.6 0.0 copy-start.3
  2.6 0.9 copy-done.3
  3.5 0.0 copy-start.4
  3.5 0.7 copy-done.4
  4.2 54.4 %blocks.1 = (bf16[2,4,64,512]{3,2,1,0:T(8,128)(2,1)S(1)}, bf16[2,4,64,2048]{3,2,1,0:T(8,128)(2,1)S(1)}, bf16[1024,2048]{1,0:T(8,128)(2,1)}) custom-call(s32[4,64]{1,0:T(4,128)S(1)} %copy-done.4, bf16[128,512]{1,0:T(8,128)(2,1)S(1)} %copy-done.3, bf16[1,2,512,2048]{3,2,1,0:T(8,128)(2,1)} %weights.1, bf16[4,64,512]{2,1,0:T(8,128)(2,1)S(1)} %copy-done.2, ...), custom_call_target="tpu_custom_call" | custom-call | tf_op jit(solution)/shard_map/blocks/pallas_call | solution.py:192
  58.6 14.1 %pack.1 = (bf16[1024,2048]{1,0:T(8,128)(2,1)}, bf16[1024,2048]{1,0:T(8,128)(2,1)}) custom-call(bf16[2,256,512]{2,1,0:T(8,128)(2,1)S(1)} %bitcast.26, bf16[2,256,2048]{2,1,0:T(8,128)(2,1)S(1)} %bitcast.24, bf16[1024,2048]{1,0:T(8,128)(2,1)} %get-tuple-element.11.shared, bf16[1024,2048]{1,0:T(8,128)(2,1)} %bitcast.28), custom_call_target="tpu_custom_call" | custom-call | tf_op jit(solution)/shard_map/pack/pallas_call | solution.py:253
  72.7 0.0 copy-start
  72.7 2.2 %copy-done = bf16[1024,2048]{1,0:T(8,128)(2,1)S(1)} copy-done((bf16[1024,2048]{1,0:T(8,128)(2,1)S(1)}, bf16[1024,2048]{1,0:T(8,128)(2,1)}, u32[]{:S(2)}) %copy-start) | copy-done | bytes 4194328
  74.9 0.0 copy-start.5
  74.9 50.8 %merge.1 = f32[128,2048]{1,0:T(8,128)S(1)} custom-call(bf16[1024,2048]{1,0:T(8,128)(2,1)S(1)} %copy-done), custom_call_target="tpu_custom_call" | custom-call | tf_op jit(solution)/shard_map/merge/pallas_call | solution.py:326
  125.7 0.0 copy-done.5
  125.7 0.0 copy-start.7
  125.7 0.9 multiply_reduce_fusion
  127.3 1.2 fusion.3
  128.5 0.0 copy-start.6
  128.5 0.0 copy-done.7
  128.5 2.6 %fusion.4 = bf16[1,128,2048]{2,1,0:T(8,128)(2,1)} fusion(bf16[1,128,2048]{2,1,0:T(8,128)(2,1)S(1)} %copy-done.7, bf16[128,2048]{1,0:T(8,128)(2,1)S(1)} %get-tuple-element.15, bf16[1024,2048]{1,0:T(8,128)(2,1)} %bitcast.27, s32[]{:T(128)S(6)} %select_n.3), kind=kLoop, calls=%fused_computation.9 | loop fusion | flops 2097152 | bytes 2097156 | tf_op jit(solution)/shard_map/broadcast_in_dim | solution.py:366
  131.1 0.0 copy-done.6
Async XLA Ops:
  0.6 1.0 copy-start.1
  1.7 0.9 copy-start.2
  2.6 0.9 copy-start.3
  3.5 0.7 copy-start.4
  72.7 2.2 %copy-start = (bf16[1024,2048]{1,0:T(8,128)(2,1)S(1)}, bf16[1024,2048]{1,0:T(8,128)(2,1)}, u32[]{:S(2)}) copy-start(bf16[1024,2048]{1,0:T(8,128)(2,1)} %get-tuple-element.12.packed) | copy-start | bytes 12582916
  74.9 50.8 %copy-start.5 = (f32[1,128,2048]{2,1,0:T(8,128)S(1)}, f32[1,128,2048]{2,1,0:T(8,128)}, u32[]{:S(2)}) copy-start(f32[1,128,2048]{2,1,0:T(8,128)} %param.14) | copy-start | bytes 3145732
  125.7 2.8 %copy-start.7 = (bf16[1,128,2048]{2,1,0:T(8,128)(2,1)S(1)}, bf16[1,128,2048]{2,1,0:T(8,128)(2,1)}, u32[]{:S(2)}) copy-start(bf16[1,128,2048]{2,1,0:T(8,128)(2,1)} %param.11) | copy-start | bytes 1572868
  128.5 2.6 %copy-start.6 = (bf16[128,2048]{1,0:T(8,128)(2,1)}, bf16[128,2048]{1,0:T(8,128)(2,1)S(1)}, u32[]{:S(2)}) copy-start(bf16[128,2048]{1,0:T(8,128)(2,1)S(1)} %get-tuple-element.15) | copy-start | bytes 1572868

commit v2 on v1

--- a/solution.py
+++ b/solution.py
@@ -37,13 +37,21 @@
 
 
 def block_kernel(
-    sections, chips, ids, embed, weights, cotangent, momentum, left, right, shared,
-    arrived, outgoing, back_arrived, back_outgoing, normed_s, scaled_s, slope_s,
-    fwd_send, fwd_recv, bwd_send, bwd_recv, own_sem, far_send, far_recv, pair_send, pair_recv,
+    sections, chips, ids, embed_in, weights_in, cotangent_in, momentum, left, right, shared,
+    embed, first_matrix, second_matrix, cotangent, load_sem, arrived, outgoing, back_arrived, back_outgoing, normed_s, scaled_s, slope_s,
+    fwd_send, fwd_recv, bwd_send, bwd_recv, own_sem, up_send, up_recv, down_send, down_recv, pair_send, pair_recv,
 ):
     micro, rows, width = cotangent.shape
     vocab = embed.shape[0]
-    channels = weights.shape[-1]
+    channels = first_matrix.shape[-1]
+    loads = [
+        pltpu.make_async_copy(embed_in, embed, load_sem.at[0]),
+        pltpu.make_async_copy(weights_in.at[0, 0], first_matrix, load_sem.at[1]),
+        pltpu.make_async_copy(weights_in.at[0, 1], second_matrix, load_sem.at[2]),
+        pltpu.make_async_copy(cotangent_in, cotangent, load_sem.at[3]),
+    ]
+    for load in loads:
+        load.start()
     tile = min(512, channels)
     owned = momentum.shape[0]
     section = lax.axis_index("section")
@@ -66,13 +74,52 @@
 
     own_copy = pltpu.make_async_copy(momentum, shared.at[span(me)], own_sem)
     own_copy.start()
-    far = []
-    for j in range(1, chips):
-        target = lax.rem(chip + j, chips) * 2 + core
-        far.append(remote(momentum, shared.at[span(me)], far_send.at[j], far_recv.at[j], dp_device(target)))
-        far[-1].start()
-    pair = [remote(momentum, shared.at[span(me)], pair_send.at[0], pair_recv.at[0], dp_device(partner))]
-    pair[0].start()
+
+    def up_copy(hop):
+        rows_of = span(me - 2 * hop)
+        source = momentum if hop == 0 else shared.at[rows_of]
+        return remote(source, shared.at[rows_of], up_send.at[hop], up_recv.at[hop], dp_device(me + 2))
+
+    def down_copy(hop):
+        rows_of = span(me + 2 * hop)
+        source = momentum if hop == 0 else shared.at[rows_of]
+        return remote(source, shared.at[rows_of], down_send.at[hop], down_recv.at[hop], dp_device(me - 2))
+
+    def pair_copy(slot, index):
+        source = momentum if slot == 0 else shared.at[span(index)]
+        return remote(source, shared.at[span(index)], pair_send.at[slot], pair_recv.at[slot], dp_device(partner))
+
+    def pass_on(hop):
+        if hop > 0:
+            @pl.when(chip >= hop)
+            def _():
+                up_copy(hop - 1).wait_recv()
+
+        @pl.when(jnp.logical_and(chip >= hop, chip < chips - 1))
+        def _():
+            up_copy(hop).start()
+
+        if hop > 0:
+            @pl.when(chip + hop < chips)
+            def _():
+                down_copy(hop - 1).wait_recv()
+
+        @pl.when(jnp.logical_and(chip + hop < chips, chip > 0))
+        def _():
+            down_copy(hop).start()
+
+        if hop == 0:
+            pair_copy(0, me).start()
+        else:
+            @pl.when(chip >= hop)
+            def _():
+                pair_copy(2 * hop - 1, me - 2 * hop).start()
+
+            @pl.when(chip + hop < chips)
+            def _():
+                pair_copy(2 * hop, me + 2 * hop).start()
+
+    pass_on(0)
 
     def fwd_copy(m):
         return remote(outgoing.at[m], arrived.at[m], fwd_send.at[m], fwd_recv.at[m], section_device(ahead))
@@ -82,12 +129,21 @@
             back_outgoing.at[m], back_arrived.at[m], bwd_send.at[m], bwd_recv.at[m], section_device(behind)
         )
 
+    loads[0].wait()
+
     @pl.when(first)
     def _():
         for m in range(micro):
             hot = ids[m : m + 1, :] == lax.broadcasted_iota(jnp.int32, (vocab, rows), 0)
             hot = jnp.where(hot, 1.0, 0.0).astype(jnp.bfloat16)
             arrived[m] = dot(hot, embed[...], TN).astype(jnp.bfloat16)
+
+    loads[1].wait()
+    loads[2].wait()
+    if chips > 2:
+        @pl.when(last)
+        def _():
+            pass_on(1)
 
     def forward(m, carry):
         @pl.when(jnp.logical_not(first))
@@ -107,7 +163,7 @@
         mixed = values
         for start in range(0, channels, tile):
             cut = slice(start, start + tile)
-            upper = dot(normed_b, weights[0, 0, :, cut])
+            upper = dot(normed_b, first_matrix[:, cut])
             square = upper * upper
             bent = jnp.tanh(gelu_coef * (upper + 0.044715 * upper * square))
             half = 0.5 * (1.0 + bent)
@@ -116,7 +172,7 @@
             slope_s[m, :, cut] = half + 0.5 * upper * (1.0 - bent * bent) * gelu_coef * (
                 1.0 + 3.0 * 0.044715 * square
             )
-            mixed = mixed + dot(hidden, weights[0, 1, :, cut], NT)
+            mixed = mixed + dot(hidden, second_matrix[:, cut], NT)
         outgoing[m] = mixed.astype(jnp.bfloat16)
 
         @pl.when(jnp.logical_not(last))
@@ -126,6 +182,12 @@
         return carry
 
     lax.fori_loop(0, micro, forward, 0)
+    loads[3].wait()
+
+    @pl.when(jnp.logical_not(last))
+    def _():
+        for hop in range(1, chips - 1):
+            pass_on(hop)
 
     def backward(m, carry):
         @pl.when(last)
@@ -141,10 +203,10 @@
         back_normed = jnp.zeros((rows, width), jnp.float32)
         for start in range(0, channels, tile):
             cut = slice(start, start + tile)
-            back_hidden = dot(grad_out, weights[0, 1, :, cut])
+            back_hidden = dot(grad_out, second_matrix[:, cut])
             back_upper = (back_hidden * slope_s[m, :, cut]).astype(jnp.bfloat16)
             right[0, m, :, cut] = back_upper
-            back_normed = back_normed + dot(back_upper, weights[0, 0, :, cut], NT)
+            back_normed = back_normed + dot(back_upper, first_matrix[:, cut], NT)
 
         @pl.when(jnp.logical_not(first))
         def _():
@@ -160,16 +222,31 @@
 
     lax.fori_loop(0, micro, backward, 0)
 
+    @pl.when(last)
+    def _():
+        for hop in range(2, chips - 1):
+            pass_on(hop)
+
+    pass_on(chips - 1)
     own_copy.wait()
-    for j in range(1, chips):
-        far[j - 1].wait()
-        origin = span(lax.rem(chip + chips - j, chips) * 2 + core)
-        pair.append(
-            remote(shared.at[origin], shared.at[origin], pair_send.at[j], pair_recv.at[j], dp_device(partner))
-        )
-        pair[-1].start()
-    for copy in pair:
-        copy.wait()
+    pair_copy(0, me).wait()
+    for hop in range(chips):
+        @pl.when(jnp.logical_and(chip >= hop, chip < chips - 1))
+        def _():
+            up_copy(hop).wait_send()
+
+        @pl.when(jnp.logical_and(chip + hop < chips, chip > 0))
+        def _():
+            down_copy(hop).wait_send()
+
+        if hop > 0:
+            @pl.when(chip >= hop)
+            def _():
+                pair_copy(2 * hop - 1, me - 2 * hop).wait()
+
+            @pl.when(chip + hop < chips)
+            def _():
+                pair_copy(2 * hop, me + 2 * hop).wait()
 
     @pl.when(jnp.logical_not(last))
     def _():
@@ -196,18 +273,22 @@
             jax.ShapeDtypeStruct((2, micro, rows, channels), jnp.bfloat16),
             jax.ShapeDtypeStruct((2 * width, channels), jnp.bfloat16),
         ),
-        in_specs=[vmem, vmem, vmem, vmem, hbm],
+        in_specs=[vmem, hbm, hbm, hbm, hbm],
         out_specs=(vmem, vmem, hbm),
         scratch_shapes=[
-            relay, relay, relay, relay,
+            pltpu.VMEM(embed.shape, jnp.bfloat16),
+            pltpu.VMEM((width, channels), jnp.bfloat16),
+            pltpu.VMEM((width, channels), jnp.bfloat16),
+            relay, dma((4,)), relay, relay, relay, relay,
             pltpu.VMEM((micro, rows, width), jnp.float32),
             pltpu.VMEM((micro, rows, 1), jnp.float32),
             pltpu.VMEM((micro, rows, channels), jnp.float32),
             dma((micro,)), dma((micro,)), dma((micro,)), dma((micro,)),
             dma, dma((chips,)), dma((chips,)), dma((chips,)), dma((chips,)),
+            dma((2 * chips,)), dma((2 * chips,)),
         ],
         compiler_params=pltpu.CompilerParams(
-            collective_id=0, has_side_effects=True, vmem_limit_bytes=48 * 1024 * 1024
+            collective_id=0, has_side_effects=True, vmem_limit_bytes=60 * 1024 * 1024
         ),
         name="blocks",
     )(ids, embed, weights, cotangent, momentum)
@@ -266,7 +347,7 @@
             pltpu.VMEM((1, channels), jnp.float32),
         ],
         compiler_params=pltpu.CompilerParams(
-            dimension_semantics=("arbitrary", "arbitrary"), vmem_limit_bytes=48 * 1024 * 1024
+            dimension_semantics=("arbitrary", "arbitrary"), vmem_limit_bytes=60 * 1024 * 1024
         ),
         name="pack",
     )(left, right, shared, error)
@@ -319,24 +400,95 @@
         total[...] += arrived[j - 1].astype(jnp.float32)
 
 
+def line_kernel(
+    chips, packed, total, own, paired, up_out, up_in, down_out, down_in,
+    own_sem, pair_send, pair_recv, up_send, up_recv, down_send, down_recv,
+):
+    owned = total.shape[0]
+    me = lax.axis_index("dp")
+    chip, core = me // 2, me % 2
+    other = 1 - core
+    partner = chip * 2 + other
+
+    barrier = pltpu.get_barrier_semaphore()
+    signal(barrier, dp_device(partner))
+    for j in range(1, chips):
+        signal(barrier, dp_device(lax.rem(chip + j, chips) * 2 + core))
+    pl.semaphore_wait(barrier, chips)
+
+    def span(index):
+        return pl.ds(pl.multiple_of(index * owned, owned), owned)
+
+    def up_copy(to):
+        return remote(up_out.at[to], up_in.at[to], up_send.at[to], up_recv.at[to], dp_device(me + 2))
+
+    def down_copy(to):
+        return remote(down_out.at[to], down_in.at[to], down_send.at[to], down_recv.at[to], dp_device(me - 2))
+
+    def at_chip(here):
+        work = [(here + chips - 1 - to, to, 0) for to in range(here, chips) if to > here or here > 0]
+        work += [(chips - 1 - here + to, to, 1) for to in range(here + 1) if to < here or here < chips - 1]
+        work.sort()
+        order = []
+        for _, to, _ in work:
+            if to != here and to not in order:
+                order.append(to)
+        order.append(here)
+        local, pair, done, started = {}, {}, set(), []
+        for to in order:
+            pair[to] = remote(
+                packed.at[span(2 * to + other)], paired.at[to], pair_send.at[to], pair_recv.at[to], dp_device(partner)
+            )
+            pair[to].start()
+            local[to] = pltpu.make_async_copy(packed.at[span(2 * to + core)], own.at[to], own_sem.at[to])
+            local[to].start()
+
+        def both(to):
+            if to not in done:
+                done.add(to)
+                local[to].wait()
+                pair[to].wait()
+            return own[to].astype(jnp.float32) + paired[to].astype(jnp.float32)
+
+        filled = False
+        for _, to, way in work:
+            copy_of, inward, outward = (down_copy, down_in, down_out) if way else (up_copy, up_in, up_out)
+            comes = here < chips - 1 if way else here > 0
+            if to == here:
+                if not filled:
+                    total[...] = both(here)
+                    filled = True
+                copy_of(to).wait_recv()
+                total[...] += inward[to].astype(jnp.float32)
+            else:
+                partial = both(to)
+                if comes:
+                    copy_of(to).wait_recv()
+                    partial = partial + inward[to].astype(jnp.float32)
+                outward[to] = partial.astype(jnp.bfloat16)
+                started.append(copy_of(to))
+                started[-1].start()
+        for copy in started:
+            copy.wait_send()
+
+    for here in range(chips):
+        pl.when(chip == here)(functools.partial(at_chip, here))
+
+
 def merge(chips, packed):
     rows, channels = packed.shape
     owned = rows // (2 * chips)
     dma = pltpu.SemaphoreType.DMA
+    line = 2 <= chips <= 4
+    block = pltpu.VMEM((chips, owned, channels), jnp.bfloat16)
     return pl.pallas_call(
-        functools.partial(merge_kernel, chips),
+        functools.partial(line_kernel if line else merge_kernel, chips),
         out_shape=jax.ShapeDtypeStruct((owned, channels), jnp.float32),
         in_specs=[pl.BlockSpec(memory_space=pl.ANY)],
         out_specs=pl.BlockSpec(memory_space=pltpu.VMEM),
-        scratch_shapes=[
-            pltpu.VMEM((chips, owned, channels), jnp.bfloat16),
-            pltpu.VMEM((chips, owned, channels), jnp.bfloat16),
-            pltpu.VMEM((chips - 1, owned, channels), jnp.bfloat16),
-            pltpu.VMEM((chips - 1, owned, channels), jnp.bfloat16),
-            dma((chips,)), dma((chips,)), dma((chips,)), dma((chips,)), dma((chips,)),
-        ],
+        scratch_shapes=[block] * (6 if line else 4) + [dma((chips,))] * (7 if line else 5),
         compiler_params=pltpu.CompilerParams(
-            collective_id=1, has_side_effects=True, vmem_limit_bytes=48 * 1024 * 1024
+            collective_id=1, has_side_effects=True, vmem_limit_bytes=60 * 1024 * 1024
         ),
         name="merge",
     )(packed)

time: 132 us -> 122 us (0.924)
  the two profiles are of different devices: /device:TPU:9 before, /device:TPU:0 now
where the time goes in v2:
time: 122 us
  Pallas kernels  113 us (93%)
  other arithmetic  7.15 us (6%)
  between operations  1.36 us (1%)
    pallas_call x1, Pallas kernels, run_blocks(): pl.pallas_call(functools.partial(block_kernel, sections, chips), out_shap...  55.1 us
    pallas_call x1, Pallas kernels, merge(): pl.pallas_call(functools.partial(line_kernel if line else merge_kernel, c...  43.7 us
    pallas_call x1, Pallas kernels, pack(): pl.pallas_call(functools.partial(pack_kernel, float(2 * width * channels)...  14.7 us
    broadcast_in_dim x1, other arithmetic, local(): (own_weights.astype(jnp.float32) - step_size).astype(jnp.bfloat16)[None]  2.55 us

profile of v2, /device:TPU:0, one launch (start us, length us, event | category | flops | bytes accessed | tf_op | source)
XLA Modules:
  0.0 121.9 jit_solution(17374009174783316042)
XLA Ops:
  0.6 55.1 %blocks.1 = (bf16[2,4,64,512]{3,2,1,0:T(8,128)(2,1)}, bf16[2,4,64,2048]{3,2,1,0:T(8,128)(2,1)}, bf16[1024,2048]{1,0:T(8,128)(2,1)}) custom-call(s32[4,64]{1,0:T(4,128)} %ids.1, bf16[128,512]{1,0:T(8,128)(2,1)} %embed_in.1, bf16[1,2,512,2048]{3,2,1,0:T(8,128)(2,1)} %weights_in.1, bf16[4,64,512]{2,1,0:T(8,128)(2,1)} %cotangent_in.1, bf16[128,2048]{1,0:T(8,128)(2,1)} %bitcast.28), custom_call_target="tpu_custom_call" | custom-call | tf_op jit(solution)/shard_map/blocks/pallas_call | solution.py:269
  55.7 14.7 %pack.1 = (bf16[1024,2048]{1,0:T(8,128)(2,1)}, bf16[1024,2048]{1,0:T(8,128)(2,1)}) custom-call(bf16[2,256,512]{2,1,0:T(8,128)(2,1)} %bitcast.29, bf16[2,256,2048]{2,1,0:T(8,128)(2,1)} %bitcast.27, bf16[1024,2048]{1,0:T(8,128)(2,1)} %get-tuple-element.11.shared, bf16[1024,2048]{1,0:T(8,128)(2,1)} %bitcast.25), custom_call_target="tpu_custom_call" | custom-call | tf_op jit(solution)/shard_map/pack/pallas_call | solution.py:334
  70.4 0.0 copy-start
  70.4 43.7 %merge.1 = f32[128,2048]{1,0:T(8,128)} custom-call(bf16[1024,2048]{1,0:T(8,128)(2,1)} %get-tuple-element.12.packed), custom_call_target="tpu_custom_call" | custom-call | tf_op jit(solution)/shard_map/merge/pallas_call | solution.py:484
  114.1 0.0 copy-done
  114.1 0.0 copy-start.2
  114.1 2.2 %multiply_reduce_fusion = f32[]{:T(128)} fusion(f32[1,128,2048]{2,1,0:T(8,128)S(1)} %copy-done, f32[128,2048]{1,0:T(8,128)} %merge.1), kind=kLoop, calls=%fused_computation.8 | loop fusion | flops 1048575 | bytes 2097156 | tf_op jit(solution)/shard_map/reduce_sum | solution.py:510
  116.9 2.4 %fusion.3 = (f32[1,128,2048]{2,1,0:T(8,128)}, bf16[128,2048]{1,0:T(8,128)(2,1)S(1)}) fusion(f32[1,128,2048]{2,1,0:T(8,128)S(1)} %copy-done, f32[128,2048]{1,0:T(8,128)} %merge.1, f32[]{:T(128)S(6)} %sqrt.7), kind=kLoop, calls=%fused_computation.5 | loop fusion | flops 1835008 | bytes 3670020 | tf_op jit(solution)/shard_map/broadcast_in_dim | solution.py:512
  119.4 0.0 copy-start.1
  119.4 0.0 copy-done.2
  119.4 2.6 %fusion.4 = bf16[1,128,2048]{2,1,0:T(8,128)(2,1)} fusion(bf16[1,128,2048]{2,1,0:T(8,128)(2,1)S(1)} %copy-done.2, bf16[128,2048]{1,0:T(8,128)(2,1)S(1)} %get-tuple-element.15, bf16[1024,2048]{1,0:T(8,128)(2,1)} %bitcast.24, s32[]{:T(128)S(6)} %select_n.3), kind=kLoop, calls=%fused_computation.9 | loop fusion | flops 2097152 | bytes 2097156 | tf_op jit(solution)/shard_map/broadcast_in_dim | solution.py:518
  121.9 0.0 copy-done.1
Async XLA Ops:
  70.4 43.7 %copy-start = (f32[1,128,2048]{2,1,0:T(8,128)S(1)}, f32[1,128,2048]{2,1,0:T(8,128)}, u32[]{:S(2)}) copy-start(f32[1,128,2048]{2,1,0:T(8,128)} %param.14) | copy-start | bytes 3145732
  114.1 5.3 %copy-start.2 = (bf16[1,128,2048]{2,1,0:T(8,128)(2,1)S(1)}, bf16[1,128,2048]{2,1,0:T(8,128)(2,1)}, u32[]{:S(2)}) copy-start(bf16[1,128,2048]{2,1,0:T(8,128)(2,1)} %param.11) | copy-start | bytes 1572868
  119.4 2.6 %copy-start.1 = (bf16[128,2048]{1,0:T(8,128)(2,1)}, bf16[128,2048]{1,0:T(8,128)(2,1)S(1)}, u32[]{:S(2)}) copy-start(bf16[128,2048]{1,0:T(8,128)(2,1)S(1)} %get-tuple-element.15) | copy-start | bytes 1572868

commit v3 on v2

--- a/solution.py
+++ b/solution.py
@@ -139,7 +139,6 @@
             arrived[m] = dot(hot, embed[...], TN).astype(jnp.bfloat16)
 
     loads[1].wait()
-    loads[2].wait()
     if chips > 2:
         @pl.when(last)
         def _():
@@ -172,7 +171,14 @@
             slope_s[m, :, cut] = half + 0.5 * upper * (1.0 - bent * bent) * gelu_coef * (
                 1.0 + 3.0 * 0.044715 * square
             )
-            mixed = mixed + dot(hidden, second_matrix[:, cut], NT)
+
+        @pl.when(m == 0)
+        def _():
+            loads[2].wait()
+
+        for start in range(0, channels, tile):
+            cut = slice(start, start + tile)
+            mixed = mixed + dot(right[1, m, :, cut], second_matrix[:, cut], NT)
         outgoing[m] = mixed.astype(jnp.bfloat16)
 
         @pl.when(jnp.logical_not(last))
@@ -200,16 +206,18 @@
             left[1, m] = back_arrived[m]
 
         grad_out = left[1, m]
-        back_normed = jnp.zeros((rows, width), jnp.float32)
         for start in range(0, channels, tile):
             cut = slice(start, start + tile)
             back_hidden = dot(grad_out, second_matrix[:, cut])
             back_upper = (back_hidden * slope_s[m, :, cut]).astype(jnp.bfloat16)
             right[0, m, :, cut] = back_upper
-            back_normed = back_normed + dot(back_upper, first_matrix[:, cut], NT)
 
         @pl.when(jnp.logical_not(first))
         def _():
+            back_normed = jnp.zeros((rows, width), jnp.float32)
+            for start in range(0, channels, tile):
+                cut = slice(start, start + tile)
+                back_normed = back_normed + dot(right[0, m, :, cut], first_matrix[:, cut], NT)
             normed = normed_s[m]
             first_mean = jnp.mean(back_normed, axis=-1, keepdims=True)
             second_mean = jnp.mean(back_normed * normed, axis=-1, keepdims=True)
@@ -494,9 +502,60 @@
     )(packed)
 
 
+def update_kernel(
+    replicas, total_in, error_in, weights_in, variance_in, new_weights, new_momentum, new_error,
+    total, error, weights, variance, sems,
+):
+    owned = new_weights.shape[1]
+    start = lax.axis_index("dp") * owned
+    rows = pl.ds(pl.multiple_of(start, owned), owned)
+    loads = [
+        pltpu.make_async_copy(total_in, total, sems.at[0]),
+        pltpu.make_async_copy(error_in.at[0], error, sems.at[1]),
+        pltpu.make_async_copy(weights_in.at[rows], weights, sems.at[2]),
+        pltpu.make_async_copy(variance_in.at[0], variance, sems.at[3]),
+    ]
+    for load in loads:
+        load.start()
+    loads[0].wait()
+    loads[1].wait()
+    merged = total[...] / replicas + error[...]
+    mean = jnp.sum(jnp.sum(merged * merged, axis=0, keepdims=True), axis=1, keepdims=True) / merged.size
+    scale = jnp.sqrt(mean + 0.01)
+    total[...] = merged
+    values = (scale * jnp.tanh(merged * (1.0 / scale))).astype(jnp.bfloat16)
+    new_momentum[0] = values
+    wide = values.astype(jnp.float32)
+    new_error[0] = total[...] - wide
+    loads[2].wait()
+    loads[3].wait()
+    step_size = 0.01 * wide / (jnp.sqrt(variance[...].astype(jnp.float32)) + 1e-08)
+    new_weights[0] = (weights[...].astype(jnp.float32) - step_size).astype(jnp.bfloat16)
+
+
+def update(replicas, total, server_error, weights, variance):
+    hbm = pl.BlockSpec(memory_space=pl.ANY)
+    vmem = pl.BlockSpec(memory_space=pltpu.VMEM)
+    narrow = jax.ShapeDtypeStruct(variance.shape, jnp.bfloat16)
+    return pl.pallas_call(
+        functools.partial(update_kernel, replicas),
+        out_shape=(narrow, narrow, jax.ShapeDtypeStruct(variance.shape, jnp.float32)),
+        in_specs=[hbm] * 4,
+        out_specs=(vmem, vmem, vmem),
+        scratch_shapes=[
+            pltpu.VMEM(total.shape, jnp.float32),
+            pltpu.VMEM(total.shape, jnp.float32),
+            pltpu.VMEM(total.shape, jnp.bfloat16),
+            pltpu.VMEM(total.shape, jnp.bfloat16),
+            pltpu.SemaphoreType.DMA((4,)),
+        ],
+        compiler_params=pltpu.CompilerParams(vmem_limit_bytes=60 * 1024 * 1024),
+        name="update",
+    )(total, server_error, weights, variance)
+
+
 def local(sections, replicas, token_ids, embed, weights, variance, momentum, worker_error, server_error, cotangent):
     width, channels = weights.shape[2:]
-    owned = 2 * width // replicas
     chips = replicas // 2
     left, right, shared = run_blocks(sections, chips, token_ids, embed, weights, cotangent, momentum[0])
     packed, new_worker = pack(
@@ -506,17 +565,10 @@
         worker_error.reshape(2 * width, channels),
     )
     total = merge(chips, packed)
-    merged = total / replicas + server_error[0]
-    server_scale = jnp.sqrt(jnp.mean(merged * merged) + 0.01)
-    server_values = (server_scale * jnp.tanh(merged / server_scale)).astype(jnp.bfloat16)
-    new_server = (merged - server_values.astype(jnp.float32))[None]
-    start = lax.axis_index("dp") * owned
-    own_weights = lax.dynamic_slice_in_dim(weights[0].reshape(2 * width, channels), start, owned, 0)
-    step_size = (
-        0.01 * server_values.astype(jnp.float32) / (jnp.sqrt(variance[0].astype(jnp.float32)) + 1e-08)
+    new_weights, new_momentum, new_server = update(
+        replicas, total, server_error, weights.reshape(2 * width, channels), variance
     )
-    new_weights = (own_weights.astype(jnp.float32) - step_size).astype(jnp.bfloat16)[None]
-    return (new_weights, server_values[None], new_worker.reshape(worker_error.shape), new_server)
+    return (new_weights, new_momentum, new_worker.reshape(worker_error.shape), new_server)
 
 
 def solution(mesh):

time: 122 us -> 117 us (0.959)
  other arithmetic: 7.15 us -> 0 us
  Pallas kernels: 113 us -> 116 us
    broadcast_in_dim x2 -> x0, other arithmetic: 4.99 us -> none  [the longest x1 2.55 us: local(): (own_weights.astype(jnp.float32) - step_size).astype(jnp.bfloat16)[None]]
    pallas_call x0 -> x1, Pallas kernels: none -> 3.6 us  [update(): pl.pallas_call(functools.partial(update_kernel, replicas), out_shape=(nar...]
    reduce_sum x1 -> x0, other arithmetic: 2.16 us -> none  [local(): server_scale = jnp.sqrt(jnp.mean(merged * merged) + 0.01)]
    pallas_call x1, Pallas kernels: 55.1 us -> 53.9 us  [run_blocks(): pl.pallas_call(functools.partial(block_kernel, sections, chips), out_shap...]
where the time goes in v3:
time: 117 us; the launch traced here: 116 us
  Pallas kernels  116 us (99%)
    pallas_call x1, Pallas kernels, run_blocks(): pl.pallas_call(functools.partial(block_kernel, sections, chips), out_shap...  53.9 us
    pallas_call x1, Pallas kernels, merge(): pl.pallas_call(functools.partial(line_kernel if line else merge_kernel, c...  43.6 us
    pallas_call x1, Pallas kernels, pack(): pl.pallas_call(functools.partial(pack_kernel, float(2 * width * channels)...  14.7 us
    pallas_call x1, Pallas kernels, update(): pl.pallas_call(functools.partial(update_kernel, replicas), out_shape=(nar...  3.6 us

profile of v3, /device:TPU:0, one launch (start us, length us, event | category | flops | bytes accessed | tf_op | source)
XLA Modules:
  0.0 116.4 jit_solution(4448618456420055526)
XLA Ops:
  0.6 53.9 %blocks.1 = (bf16[2,4,64,512]{3,2,1,0:T(8,128)(2,1)}, bf16[2,4,64,2048]{3,2,1,0:T(8,128)(2,1)}, bf16[1024,2048]{1,0:T(8,128)(2,1)}) custom-call(s32[4,64]{1,0:T(4,128)} %ids.1, bf16[128,512]{1,0:T(8,128)(2,1)} %embed_in.1, bf16[1,2,512,2048]{3,2,1,0:T(8,128)(2,1)} %weights_in.1, bf16[4,64,512]{2,1,0:T(8,128)(2,1)} %cotangent_in.1, bf16[128,2048]{1,0:T(8,128)(2,1)} %bitcast.9), custom_call_target="tpu_custom_call" | custom-call | tf_op jit(solution)/shard_map/blocks/pallas_call | solution.py:277
  54.5 14.7 %pack.1 = (bf16[1024,2048]{1,0:T(8,128)(2,1)}, bf16[1024,2048]{1,0:T(8,128)(2,1)}) custom-call(bf16[2,256,512]{2,1,0:T(8,128)(2,1)} %bitcast.10, bf16[2,256,2048]{2,1,0:T(8,128)(2,1)} %bitcast.8, bf16[1024,2048]{1,0:T(8,128)(2,1)} %get-tuple-element.14.shared, bf16[1024,2048]{1,0:T(8,128)(2,1)} %bitcast.7), custom_call_target="tpu_custom_call" | custom-call | tf_op jit(solution)/shard_map/pack/pallas_call | solution.py:342
  69.2 43.6 %merge.1.total_in = f32[128,2048]{1,0:T(8,128)} custom-call(bf16[1024,2048]{1,0:T(8,128)(2,1)} %get-tuple-element.15.packed), custom_call_target="tpu_custom_call" | custom-call | tf_op jit(solution)/shard_map/merge/pallas_call | solution.py:492
  112.8 3.6 %update.1 = (bf16[1,128,2048]{2,1,0:T(8,128)(2,1)}, bf16[1,128,2048]{2,1,0:T(8,128)(2,1)}, f32[1,128,2048]{2,1,0:T(8,128)}) custom-call(f32[128,2048]{1,0:T(8,128)} %merge.1.total_in, f32[1,128,2048]{2,1,0:T(8,128)} %error_in.1, bf16[1024,2048]{1,0:T(8,128)(2,1)} %bitcast.6, bf16[1,128,2048]{2,1,0:T(8,128)(2,1)} %variance_in.1), custom_call_target="tpu_custom_call" | custom-call | tf_op jit(solution)/shard_map/update/pallas_call | solution.py:540

commit v4 on v3

--- a/solution.py
+++ b/solution.py
@@ -329,7 +329,7 @@
 def pack(left, right, shared, error):
     _, tokens, width = left.shape
     channels = right.shape[-1]
-    tile = 128
+    tile = min(256, width)
     per = width // tile
     steps = 2 * per
 
@@ -418,14 +418,20 @@
     other = 1 - core
     partner = chip * 2 + other
 
+    def span(index):
+        return pl.ds(pl.multiple_of(index * owned, owned), owned)
+
+    def own_copy(to):
+        return pltpu.make_async_copy(packed.at[span(2 * to + core)], own.at[to], own_sem.at[to])
+
+    for to in range(chips):
+        own_copy(to).start()
+
     barrier = pltpu.get_barrier_semaphore()
     signal(barrier, dp_device(partner))
     for j in range(1, chips):
         signal(barrier, dp_device(lax.rem(chip + j, chips) * 2 + core))
     pl.semaphore_wait(barrier, chips)
-
-    def span(index):
-        return pl.ds(pl.multiple_of(index * owned, owned), owned)
 
     def up_copy(to):
         return remote(up_out.at[to], up_in.at[to], up_send.at[to], up_recv.at[to], dp_device(me + 2))
@@ -442,19 +448,17 @@
             if to != here and to not in order:
                 order.append(to)
         order.append(here)
-        local, pair, done, started = {}, {}, set(), []
+        pair, done, started = {}, set(), []
         for to in order:
             pair[to] = remote(
                 packed.at[span(2 * to + other)], paired.at[to], pair_send.at[to], pair_recv.at[to], dp_device(partner)
             )
             pair[to].start()
-            local[to] = pltpu.make_async_copy(packed.at[span(2 * to + core)], own.at[to], own_sem.at[to])
-            local[to].start()
 
         def both(to):
             if to not in done:
                 done.add(to)
-                local[to].wait()
+                own_copy(to).wait()
                 pair[to].wait()
             return own[to].astype(jnp.float32) + paired[to].astype(jnp.float32)
 

time: 117 us -> 114 us (0.974)
  Pallas kernels: 116 us -> 113 us
    pallas_call x1, Pallas kernels: 14.7 us -> 12 us  [pack(): pl.pallas_call(functools.partial(pack_kernel, float(2 * width * channels)...]
where the time goes in v4:
time: 114 us
  Pallas kernels  113 us (99%)
    pallas_call x1, Pallas kernels, run_blocks(): pl.pallas_call(functools.partial(block_kernel, sections, chips), out_shap...  53.9 us
    pallas_call x1, Pallas kernels, merge(): pl.pallas_call(functools.partial(line_kernel if line else merge_kernel, c...  43.7 us
    pallas_call x1, Pallas kernels, pack(): pl.pallas_call(functools.partial(pack_kernel, float(2 * width * channels)...  12 us
    pallas_call x1, Pallas kernels, update(): pl.pallas_call(functools.partial(update_kernel, replicas), out_shape=(nar...  3.6 us

profile of v4, /device:TPU:0, one launch (start us, length us, event | category | flops | bytes accessed | tf_op | source)
XLA Modules:
  0.0 113.8 jit_solution(1866007779617666882)
XLA Ops:
  0.6 53.9 %blocks.1 = (bf16[2,4,64,512]{3,2,1,0:T(8,128)(2,1)}, bf16[2,4,64,2048]{3,2,1,0:T(8,128)(2,1)}, bf16[1024,2048]{1,0:T(8,128)(2,1)}) custom-call(s32[4,64]{1,0:T(4,128)} %ids.1, bf16[128,512]{1,0:T(8,128)(2,1)} %embed_in.1, bf16[1,2,512,2048]{3,2,1,0:T(8,128)(2,1)} %weights_in.1, bf16[4,64,512]{2,1,0:T(8,128)(2,1)} %cotangent_in.1, bf16[128,2048]{1,0:T(8,128)(2,1)} %bitcast.9), custom_call_target="tpu_custom_call" | custom-call | tf_op jit(solution)/shard_map/blocks/pallas_call | solution.py:277
  54.5 12.0 %pack.1 = (bf16[1024,2048]{1,0:T(8,128)(2,1)}, bf16[1024,2048]{1,0:T(8,128)(2,1)}) custom-call(bf16[2,256,512]{2,1,0:T(8,128)(2,1)} %bitcast.10, bf16[2,256,2048]{2,1,0:T(8,128)(2,1)} %bitcast.8, bf16[1024,2048]{1,0:T(8,128)(2,1)} %get-tuple-element.14.shared, bf16[1024,2048]{1,0:T(8,128)(2,1)} %bitcast.7), custom_call_target="tpu_custom_call" | custom-call | tf_op jit(solution)/shard_map/pack/pallas_call | solution.py:342
  66.6 43.7 %merge.1.total_in = f32[128,2048]{1,0:T(8,128)} custom-call(bf16[1024,2048]{1,0:T(8,128)(2,1)} %get-tuple-element.15.packed), custom_call_target="tpu_custom_call" | custom-call | tf_op jit(solution)/shard_map/merge/pallas_call | solution.py:496
  110.2 3.6 %update.1 = (bf16[1,128,2048]{2,1,0:T(8,128)(2,1)}, bf16[1,128,2048]{2,1,0:T(8,128)(2,1)}, f32[1,128,2048]{2,1,0:T(8,128)}) custom-call(f32[128,2048]{1,0:T(8,128)} %merge.1.total_in, f32[1,128,2048]{2,1,0:T(8,128)} %error_in.1, bf16[1024,2048]{1,0:T(8,128)(2,1)} %bitcast.6, bf16[1,128,2048]{2,1,0:T(8,128)(2,1)} %variance_in.1), custom_call_target="tpu_custom_call" | custom-call | tf_op jit(solution)/shard_map/update/pallas_call | solution.py:544
